TPU v7x, 32 devices: a whole 2x2x4 slice. The times are simulated.
32 devices in a mesh: group: 4 (over x, core), prompt: 8 (over z, y).
Axes of the slice: x: 2, y: 2, z: 4, core: 2. Of those that a mesh axis runs over, the one named last changes fastest.
Arguments:
- queries: bfloat16 [8, 4, 64, 3072], P('prompt', 'group'), may hold values from -48 to 48
- fresh_latent: bfloat16 [8, 4, 64, 576], P('prompt', 'group'), may hold values from -6 to 6
- latent_cache: bfloat16 [8, 4, 512, 576], P('prompt', 'group'), may hold values from -48 to 48
- selected: int32 [8, 4, 64], P('prompt', 'group'), may hold values from 0 to 511, as said below
- position: int32 [8, 4], P('prompt'), may hold values from 0 to 3, each once within a row
- latent_gain: bfloat16 [512], replicated, may hold values from 0.099609375 to 1.8984375
- kv_up: bfloat16 [512, 4096], P('prompt'), may hold values from -0.25 to 0.25
- out_weight: bfloat16 [2048, 2048], P('prompt'), may hold values from -0.125 to 0.125
Outputs:
- attended: bfloat16 [8, 4, 64, 2048], P('prompt', 'group')
- blended: bfloat16 [8, 4, 512, 576], P('prompt', 'group')
Inputs may be any that keep to these rules, and one draw needn't show every extreme that they name: `selected`: the 64 indices of a group are distinct and increasing.
All inputs are finite; a program needn't handle non-finite values.
Results may differ from a plain program's by a relative error of at most 0.011.
Values may be sent and summed in bfloat16 or wider, within the bound.
No kernel may reach another device: no remote copies, remote signals or barrier semaphores. Data moves between devices by JAX's collectives and lax.ppermute only.
A program may use at most 128 MiB of HBM per device.

v0:
```python
import jax
import jax.numpy as jnp
from jax import lax
from jax.sharding import PartitionSpec as P

D = 2048
H = 16
DN = 128
DR = 64
DV = 128
LAT = 512


def rope_rotate(values, places):
    half = values.shape[-1] // 2
    freqs = 10000.0 ** (-jnp.arange(half, dtype=jnp.float32) / half)
    angles = places[..., None] * freqs
    cosine = jnp.cos(angles)
    sine = jnp.sin(angles)
    first = values[..., :half]
    second = values[..., half:]
    return jnp.concatenate([first * cosine - second * sine, second * cosine + first * sine], -1)


def prepare_rows(fresh, gain, places):
    latent = fresh[..., :LAT].astype(jnp.float32)
    factor = lax.rsqrt(jnp.mean(latent * latent, -1, keepdims=True) + 1e-06)
    normed = latent * factor * gain.astype(jnp.float32)
    turned = rope_rotate(fresh[..., LAT:].astype(jnp.float32), places)
    return jnp.concatenate([normed, turned], -1).astype(jnp.bfloat16)


def shards(queries, fresh_latent, latent_cache, selected, position, latent_gain, kv_up, out_weight):
    prompts, groups, picks, _ = queries.shape
    length = latent_cache.shape[2]
    first_group = lax.axis_index("group") * groups
    own_order = lax.dynamic_slice_in_dim(position, first_group, groups, 1)
    place_int = own_order[:, :, None] * length + selected
    places = place_int.astype(jnp.float32)
    fresh_rows = prepare_rows(fresh_latent, latent_gain, places)
    prompt_ids = jnp.arange(prompts, dtype=jnp.int32)[:, None, None]
    group_ids = jnp.arange(groups, dtype=jnp.int32)[None, :, None]
    blended = latent_cache.at[prompt_ids, group_ids, selected].set(fresh_rows)
    whole_kv = lax.all_gather(kv_up, "prompt", axis=0, tiled=True).reshape(LAT, H, DN + DV)
    shaped = queries.reshape(prompts, groups, picks, H, DN + DR)
    absorbed = jnp.einsum(
        "pcshd,lhd->pcshl", shaped[..., :DN], whole_kv[..., :DN], preferred_element_type=jnp.float32
    ).astype(jnp.bfloat16)
    turned = rope_rotate(shaped[..., DN:].astype(jnp.float32), places[..., None]).astype(
        jnp.bfloat16
    )
    rows = groups * picks
    query_vec = jnp.concatenate([absorbed, turned], -1).reshape(prompts, rows, H, LAT + DR)
    query_place = place_int.reshape(prompts, rows)
    scale = (DN + DR) ** (-0.5)
    offsets = jnp.arange(length, dtype=jnp.int32)

    def update(state, keys, key_place):
        peak, total, mixed = state
        allowed = (key_place[:, None, :] <= query_place[:, :, None])[:, :, None, :]
        scores = (
            jnp.einsum("pqhe,pke->pqhk", query_vec, keys, preferred_element_type=jnp.float32)
            * scale
        )
        block_peak = jnp.max(jnp.where(allowed, scores, -1e30), -1)
        new_peak = jnp.maximum(peak, block_peak)
        probs = jnp.where(allowed, jnp.exp(scores - new_peak[..., None]), 0.0)
        decay = jnp.exp(peak - new_peak)
        total = total * decay + jnp.sum(probs, -1)
        mixed = mixed * decay[..., None] + jnp.einsum(
            "pqhk,pkl->pqhl",
            probs.astype(jnp.bfloat16),
            keys[..., :LAT],
            preferred_element_type=jnp.float32,
        )
        return (new_peak, total, mixed)

    start_state = (
        jnp.full((prompts, rows, H), -1e30, jnp.float32),
        jnp.zeros((prompts, rows, H), jnp.float32),
        jnp.zeros((prompts, rows, H, LAT), jnp.float32),
    )
    piece = lax.all_gather(blended, "group", axis=1, tiled=True)

    def one_group(index, carry):
        keys = lax.dynamic_slice_in_dim(piece, index, 1, 1)[:, 0]
        order = lax.dynamic_slice_in_dim(position, index, 1, 1)
        key_place = order * length + offsets[None, :]
        needed = jnp.any(key_place[:, :1] <= jnp.max(query_place, -1, keepdims=True))
        return lax.cond(needed, lambda c: update(c, keys, key_place), lambda c: c, carry)

    peak, total, mixed = lax.fori_loop(0, piece.shape[1], one_group, start_state)
    latent_mix = (mixed / total[..., None]).astype(jnp.bfloat16)
    heads = jnp.einsum(
        "pqhl,lhv->pqhv", latent_mix, whole_kv[..., DN:], preferred_element_type=jnp.float32
    ).astype(jnp.bfloat16)
    heads = heads.reshape(prompts * rows, H * DV)
    whole_out = lax.all_gather(out_weight, "prompt", axis=0, tiled=True)
    attended = jnp.dot(heads, whole_out, preferred_element_type=jnp.float32)
    return (attended.astype(jnp.bfloat16).reshape(prompts, groups, picks, D), blended)


def solution(mesh):
    in_specs = (
        P("prompt", "group", None, None),
        P("prompt", "group", None, None),
        P("prompt", "group", None, None),
        P("prompt", "group", None),
        P("prompt", None),
        P(),
        P("prompt", None),
        P("prompt", None),
    )
    out_specs = (P("prompt", "group", None, None), P("prompt", "group", None, None))
    return jax.shard_map(shards, mesh=mesh, in_specs=in_specs, out_specs=out_specs, check_vma=False)
```

profile of v0, /device:TPU:0, one launch (start us, length us, event | category | flops | bytes accessed | tf_op | source)
XLA Modules:
  0.0 257.9 jit_solution(10808461061996770025)
XLA Ops:
  7.2 0.0 all-gather.9.cloned.1.call-start
  7.2 0.8 slice.44
  8.0 1.0 fusion.33
  8.9 0.1 copy.63
  9.0 1.2 fusion.52
  10.3 1.3 convert_bitcast_fusion
  11.6 0.1 fusion.46
  11.7 0.1 copy.51
  11.8 0.1 copy.52
  12.0 0.0 copy-start.4
  12.0 1.4 copy.49
  13.4 0.7 convert_element_type.80
  14.1 0.9 fusion.35
  15.0 1.3 scatter_custom_fusion
  16.4 0.8 copy-done.1
  17.2 0.0 all-gather.9.cloned.1.call-update
  17.2 0.0 copy-start.2
  17.2 0.0 all-gather.5.cloned.1.call-start
  17.3 0.7 all-gather.5.cloned.1.call-update
  18.0 0.0 all-gather.7.cloned.1.call-start
  18.0 0.7 all-gather.7.cloned.1.call-update
  18.7 0.6 reshape.418
  19.4 1.1 copy.62
  20.5 0.7 reduce_max.22
  21.2 0.2 multiply_cosine_fusion
  21.4 0.1 copy_convert_fusion
  21.4 0.3 subtract_convert_fusion
  21.7 23.9 %all-gather.9.cloned.1.call-done = bf16[2048,576]{1,0:T(8,128)(2,1)} async-done(((bf16[512,576]{1,0:T(8,128)(2,1)}), bf16[2048,576]{1,0:T(8,128)(2,1)}) %all-gather.9.cloned.1.call-update) | async-done | bytes 2359312 | tf_op jit(solution)/shard_map/all_gather | solution.py:83
  45.6 4.3 %copy.57 = bf16[1,4,512,576]{2,3,1,0:T(8,128)(2,1)} copy(bf16[1,4,512,576]{3,2,1,0:T(8,128)(2,1)} %bitcast.104) | data formatting | bytes 4718592
  49.9 70.6 %all-gather.5.cloned.1.call-done = bf16[512,4096]{1,0:T(8,128)(2,1)} async-done(((bf16[64,4096]{1,0:T(8,128)(2,1)}), bf16[512,4096]{1,0:T(8,128)(2,1)}) %all-gather.5.cloned.1.call-update) | async-done | bytes 4194320 | tf_op jit(solution)/shard_map/all_gather | solution.py:44
  120.6 6.5 %copy.53 = bf16[512,4096]{0,1:T(8,128)(2,1)} copy(bf16[512,4096]{1,0:T(8,128)(2,1)} %all-gather.5.cloned.1.call-done) | data formatting | bytes 8388608 | tf_op jit(solution)/shard_map/all_gather | solution.py:44
  127.1 0.0 slice-done
  127.1 2.2 fusion.20
  129.3 0.0 copy-start.5
  129.3 1.3 maximum_bitcast_fusion
  130.6 0.2 broadcast_in_dim.55
  130.9 20.7 %while.20 = (s32[]{:T(128)}, f32[1,64,16]{1,2,0:T(8,128)S(1)}, f32[1,64,16]{1,2,0:T(8,128)S(1)}, f32[1,64,16,512]{3,2,1,0:T(8,128)S(1)}, s32[1,4]{1,0:T(1,128)S(...) while((s32[]{:T(128)}, f32[1,64,16]{1,2,0:T(8,128)S(1)}, ...), condition=%wide.region_8.9_spmd.clone, body=%wide.region_3.8_spmd.clone.sunk | while | flops 1146129920 | bytes 17670692 | solution.py:92
  130.9 0.6 fusion.55
  131.5 0.6 iota_add_fusion.2
  132.1 0.5 slice.101
  133.8 9.0 %conditional.3 = ((f32[1,64,16]{1,2,0:T(8,128)S(1)}, f32[1,64,16]{1,2,0:T(8,128)S(1)}, f32[1,64,16,512]{3,2,1,0:T(8,128)S(1)})) conditional(s32[]{:T(128)} %bitcast.97, (f32[1,64,16]{1,2,0:T(8,128)S(1)}, f32[1,64,16]{1,2,0:T(8,128)S(1)}, f32[1,64,16,512]{3,2,1,0:T(8,128)S(1)}) %tuple.70, (s32[1,512]{1,0:T(1,128)S(1)}, s32[1,1,64]{2,1,0:T(1,128)S(1)}, ...), branch_computations={%region_4.0_spmd, %region_5.7_spmd} | conditional | flops 1146129408 | bytes 17668416 | solution.py:90
  133.8 1.1 constant_dynamic-slice_fusion
  135.0 0.0 copy-start
  135.0 0.1 broadcast_compare_fusion
  135.1 2.5 fusion.2
  137.6 0.7 fusion.5
  138.3 0.1 copy.46
  138.4 2.1 copy.47
  140.5 2.2 bitcast_add_fusion
  142.8 0.6 fusion.55
  143.4 0.6 iota_add_fusion.2
  144.0 0.5 slice.101
  145.8 0.6 fusion.55
  146.3 0.6 iota_add_fusion.2
  146.9 0.5 slice.101
  148.7 0.6 fusion.55
  149.3 0.6 iota_add_fusion.2
  149.9 0.5 slice.101
  151.7 0.1 copy.58
  151.7 0.2 fusion.30
  152.0 2.4 fusion.26
  154.4 0.2 copy.61
  154.6 91.2 %all-gather.7.cloned.1.call-done = bf16[2048,2048]{1,0:T(8,128)(2,1)} async-done(((bf16[256,2048]{1,0:T(8,128)(2,1)}), bf16[2048,2048]{1,0:T(8,128)(2,1)}) %all-gather.7.cloned.1.call-update) | async-done | bytes 8388624 | tf_op jit(solution)/shard_map/all_gather | solution.py:98
  245.7 5.7 %fusion.12 = bf16[1,1,64,2048]{3,2,1,0:T(8,128)(2,1)} fusion(bf16[2048,2048]{1,0:T(8,128)(2,1)} %all-gather.7.cloned.1.call-done, bf16[8,8,16,128]{3,2,1,0:T(8,128)(2,1)S(1)} %bitcast.105), kind=kOutput, calls=%fused_computation.24 | convolution fusion | flops 537001984 | bytes 8912896 | tf_op jit(solution)/shard_map/dot_general | solution.py:99
  (22 shorter events, 0.2 us)
Async XLA Ops:
  7.2 38.5 %all-gather.9.cloned.1.call-start = ((), (), s32[]{:S(2)}) async-start(), calls=%async_computation.2 | async-start | bytes 3276800 | tf_op jit(solution)/shard_map/all_gather | solution.py:83
  12.0 6.7 %copy-start.4 = (bf16[1,1,64,3072]{3,2,1,0:T(8,128)(2,1)S(1)}, bf16[1,1,64,3072]{3,2,1,0:T(8,128)(2,1)}, u32[]{:S(2)}) copy-start(bf16[1,1,64,3072]{3,2,1,0:T(8,128)(2,1)} %param.12) | copy-start | bytes 1179652
  16.3 0.8 copy-start.1
  17.2 2.2 copy-start.2
  17.2 103.4 %all-gather.5.cloned.1.call-start = ((), (), s32[]{:S(2)}) async-start(), calls=%async_computation | async-start | bytes 4718592 | tf_op jit(solution)/shard_map/all_gather | solution.py:44
  18.0 227.8 %all-gather.7.cloned.1.call-start = ((), (), s32[]{:S(2)}) async-start(), calls=%async_computation.1 | async-start | bytes 9437184 | tf_op jit(solution)/shard_map/all_gather | solution.py:98
  19.3 2.4 copy-start.3
  49.9 77.1 %slice-start = ((bf16[1,1,64,16,192]{4,3,2,1,0:T(8,128)(2,1)}), bf16[1,1,64,16,128]{4,3,2,1,0:T(8,128)(2,1)S(1)}, s32[]{:S(2)}) async-start(bf16[1,1,64,16,192]{4,3,2,1,0:T(8,128)(2,1)} %copy-done.3), calls=%async_computation.3 | async-start | bytes 524288 | tf_op jit(solution)/shard_map/slice | solution.py:47
  129.3 1.6 copy-start.5
  135.0 2.6 %copy-start = (bf16[1,1,512,576]{2,3,1,0:T(8,128)(2,1)}, bf16[1,1,512,576]{2,3,1,0:T(8,128)(2,1)S(1)}, u32[]{:S(2)}) copy-start(bf16[1,1,512,576]{2,3,1,0:T(8,128)(2,1)S(1)} %constant_dynamic-slice_fusion) | copy-start | bytes 1769476 | tf_op jit(solution)/shard_map/while/body/eval_jaxpr/cond
Sparse Core Ops, SparseCore 0:
  17.3 28.2 all-gather.8
  47.7 72.7 all-gather.4
  122.7 122.9 all-gather.6
where the time goes:
time: 259 us; the launch traced here: 258 us
  waiting for transfers between devices  187 us (72%)
  local copies, waits for them, and re-layouts  21.7 us (8%)
  matrix products  15 us (6%)
  other arithmetic  14.7 us (6%)
  between operations  14 us (5%)
  loops' own time  5.23 us (2%)
    all_gather x1, waiting for transfers between devices, shards(): whole_out = lax.all_gather(out_weight, 'prompt', axis=0, tiled=True)  91.2 us
    all_gather x1, waiting for transfers between devices, shards(): lax.all_gather(kv_up, 'prompt', axis=0, tiled=True).reshape(LAT, H, DN + DV)  70.6 us
    all_gather x1, waiting for transfers between devices, shards(): piece = lax.all_gather(blended, 'group', axis=1, tiled=True)  23.9 us
    unnamed x14, local copies, waits for them, and re-layouts  7.73 us
    all_gather x1, local copies, waits for them, and re-layouts, shards(): lax.all_gather(kv_up, 'prompt', axis=0, tiled=True).reshape(LAT, H, DN + DV)  6.48 us
    dot_general x1, matrix products, shards(): attended = jnp.dot(heads, whole_out, preferred_element_type=jnp.float32)  5.65 us
  transfers between devices with their start and end apart: 3, of which 3 were waited for; matrix products, arithmetic and copies ran while one was open for 14% of the time, Pallas kernels for 0%

commit v1 on v0

--- a/solution.py
+++ b/solution.py
@@ -9,6 +9,17 @@
 DR = 64
 DV = 128
 LAT = 512
+
+
+def turned_line(x, mesh_axis, d):
+    size = lax.axis_size(mesh_axis)
+    right = [(i, (i + 1) % size) for i in range(size)]
+    shards = [x]
+    for hop in range(1, size):
+        shards = [lax.ppermute(shards[0], mesh_axis, right), *shards]
+    whole = jnp.concatenate(shards, axis=d)
+    turn = (lax.axis_index(mesh_axis) + 1) * shards[-1].shape[d]
+    return jnp.roll(whole, turn, axis=d)
 
 
 def rope_rotate(values, places):
@@ -80,7 +91,7 @@
         jnp.zeros((prompts, rows, H), jnp.float32),
         jnp.zeros((prompts, rows, H, LAT), jnp.float32),
     )
-    piece = lax.all_gather(blended, "group", axis=1, tiled=True)
+    piece = turned_line(blended, "group", 1)
 
     def one_group(index, carry):
         keys = lax.dynamic_slice_in_dim(piece, index, 1, 1)[:, 0]

time: 259 us -> 225 us (0.87)
  waiting for transfers between devices: 187 us -> 154 us
    all_gather x1, waiting for transfers between devices: 70.6 us -> 36.3 us  [shards(): lax.all_gather(kv_up, 'prompt', axis=0, tiled=True).reshape(LAT, H, DN + DV)]
    ppermute x0 -> x3, waiting for transfers between devices: none -> 25.1 us  [turned_line(): shards = [lax.ppermute(shards[0], mesh_axis, right), *shards]]
    all_gather x1 -> x0, waiting for transfers between devices: 23.9 us -> none  [shards(): piece = lax.all_gather(blended, 'group', axis=1, tiled=True)]
    unnamed x14 -> x24, local copies, waits for them, and re-layouts: 7.73 us -> 4.67 us
  transfers between devices with their start and end apart: 3 -> 5, of which waited for: 3 -> 5; matrix products, arithmetic and copies ran while one was open for 14% -> 20% of each run, Pallas kernels for 0% -> 0%
where the time goes in v1:
time: 225 us; the launch traced here: 223 us
  waiting for transfers between devices  154 us (68%)
  local copies, waits for them, and re-layouts  21.2 us (9%)
  matrix products  15.1 us (7%)
  between operations  14.4 us (6%)
  other arithmetic  13.3 us (6%)
  loops' own time  5.04 us (2%)
    all_gather x1, waiting for transfers between devices, shards(): whole_out = lax.all_gather(out_weight, 'prompt', axis=0, tiled=True)  91 us
    all_gather x1, waiting for transfers between devices, shards(): lax.all_gather(kv_up, 'prompt', axis=0, tiled=True).reshape(LAT, H, DN + DV)  36.3 us
    ppermute x3, waiting for transfers between devices, turned_line(): shards = [lax.ppermute(shards[0], mesh_axis, right), *shards]  25.1 us
    all_gather x1, local copies, waits for them, and re-layouts, shards(): lax.all_gather(kv_up, 'prompt', axis=0, tiled=True).reshape(LAT, H, DN + DV)  6.47 us
    dot_general x1, matrix products, shards(): attended = jnp.dot(heads, whole_out, preferred_element_type=jnp.float32)  5.65 us
    another operation x1, loops' own time, shards(): lax.fori_loop(0, piece.shape[1], one_group, start_state)  4.92 us
    unnamed x24, local copies, waits for them, and re-layouts  4.67 us
  transfers between devices with their start and end apart: 5, of which 5 were waited for; matrix products, arithmetic and copies ran while one was open for 20% of the time, Pallas kernels for 0%

profile of v1, /device:TPU:0, one launch (start us, length us, event | category | flops | bytes accessed | tf_op | source)
XLA Modules:
  0.0 223.3 jit_solution(17424806439999960745)
XLA Ops:
  7.2 0.7 all-gather.3.cloned.1.call-update
  8.0 0.7 all-gather.5.cloned.1.call-update
  8.7 0.7 slice.44
  9.4 0.1 copy.76
  9.5 1.2 fusion.52
  10.8 1.3 convert_bitcast_fusion
  12.1 0.2 fusion.46
  12.3 0.1 copy.57
  12.4 0.1 copy.58
  12.5 1.4 copy.55
  13.9 0.1 fusion.33
  14.1 1.3 scatter_custom_fusion
  15.4 0.2 copy.59
  15.7 0.5 collective-permute-start
  16.2 9.5 %collective-permute-done = bf16[1,1,512,576]{2,3,1,0:T(8,128)(2,1)S(1)} collective-permute-done((bf16[1,1,512,576]{2,3,1,0:T(8,128)(2,1)S(1)}, bf16[1,1,512,576]{2,3,1,0:T(8,128)(2,1)S(1)}, u32[]{:S(2)}, u32[]{:S(2)}) %collective-permute-start) | collective-permute-done | bytes 589856 | tf_op jit(solution)/shard_map/ppermute | solution.py:19
  25.7 9.3 %collective-permute-done.1 = bf16[1,1,512,576]{2,3,1,0:T(8,128)(2,1)S(1)} collective-permute-done((bf16[1,1,512,576]{2,3,1,0:T(8,128)(2,1)S(1)}, bf16[1,1,512,576]{2,3,1,0:T(8,128)(2,1)S(1)}, u32[]{:S(2)}, u32[]{:S(2)}) %collective-permute-start.1) | collective-permute-done | bytes 589856 | tf_op jit(solution)/shard_map/ppermute | solution.py:19
  35.0 0.2 multiply_cosine_fusion
  35.2 0.6 reshape.418
  35.9 0.6 reduce_max.22
  36.6 0.9 subtract_convert_fusion
  37.5 0.3 copy.62
  37.8 0.3 copy.61
  38.1 6.3 %collective-permute-done.2 = bf16[1,1,512,576]{2,3,1,0:T(8,128)(2,1)} collective-permute-done((bf16[1,1,512,576]{2,3,1,0:T(8,128)(2,1)S(1)}, bf16[1,1,512,576]{2,3,1,0:T(8,128)(2,1)}, u32[]{:S(2)}, u32[]{:S(2)}) %collective-permute-start.2) | collective-permute-done | bytes 589856 | tf_op jit(solution)/shard_map/ppermute | solution.py:19
  44.4 1.4 copy.60
  45.9 0.1 constant_dynamic-update-slice_fusion.6
  46.0 0.1 constant_dynamic-update-slice_fusion.5
  46.1 0.1 constant_dynamic-update-slice_fusion.4
  46.2 0.1 constant_dynamic-update-slice_fusion.3
  46.3 0.1 constant_dynamic-update-slice_fusion.2
  46.4 0.1 constant_dynamic-update-slice_fusion.1
  46.5 0.1 constant_dynamic-update-slice_fusion
  46.6 0.2 constant_dynamic-slice_fusion.2
  46.8 2.5 %copy.70 = bf16[1,4,512,576]{2,3,1,0:T(8,128)(2,1)} copy(bf16[1,4,512,576]{3,2,1,0:T(8,128)(2,1)S(1)} %constant_dynamic-slice_fusion.2) | data formatting | bytes 4718592
  49.4 36.3 %all-gather.3.cloned.1.call-done = bf16[512,4096]{1,0:T(8,128)(2,1)} async-done(((bf16[64,4096]{1,0:T(8,128)(2,1)}), bf16[512,4096]{1,0:T(8,128)(2,1)}) %all-gather.3.cloned.1.call-update) | async-done | bytes 4194320 | tf_op jit(solution)/shard_map/all_gather | solution.py:55
  85.7 6.5 %copy.66 = bf16[512,4096]{0,1:T(8,128)(2,1)} copy(bf16[512,4096]{1,0:T(8,128)(2,1)} %all-gather.3.cloned.1.call-done) | data formatting | bytes 8388608 | tf_op jit(solution)/shard_map/all_gather | solution.py:55
  92.1 2.2 %fusion.20 = bf16[1,1,64,16,512]{4,2,3,1,0:T(8,128)(2,1)S(1)} fusion(bf16[512,16,256]{0,2,1:T(8,128)(2,1)} %bitcast.102, bf16[1,1,64,16,128]{4,3,2,1,0:T(8,128)(2,1)S(1)} %slice-done), kind=kOutput, calls=%fused_computation.31 | convolution fusion | flops 134742016 | bytes 3407872 | tf_op jit(solution)/shard_map/pcshd,lhd->pcshl/dot_general | solution.py:57
  94.4 1.3 maximum_bitcast_fusion
  95.8 0.2 broadcast_in_dim.55
  96.0 20.9 %while.20 = (s32[]{:T(128)}, f32[1,64,16]{1,2,0:T(8,128)S(1)}, f32[1,64,16]{1,2,0:T(8,128)S(1)}, f32[1,64,16,512]{3,2,1,0:T(8,128)S(1)}, s32[1,4]{1,0:T(1,128)S(...) while((s32[]{:T(128)}, f32[1,64,16]{1,2,0:T(8,128)S(1)}, ...), condition=%wide.region_8.9_spmd.clone, body=%wide.region_3.8_spmd.clone.sunk | while | flops 1146129920 | bytes 17670692 | solution.py:103
  96.1 0.6 fusion.55
  96.6 0.6 iota_add_fusion.2
  97.3 0.5 slice.101
  99.0 9.0 %conditional.3 = ((f32[1,64,16]{1,2,0:T(8,128)S(1)}, f32[1,64,16]{1,2,0:T(8,128)S(1)}, f32[1,64,16,512]{3,2,1,0:T(8,128)S(1)})) conditional(s32[]{:T(128)} %bitcast.98, (f32[1,64,16]{1,2,0:T(8,128)S(1)}, f32[1,64,16]{1,2,0:T(8,128)S(1)}, f32[1,64,16,512]{3,2,1,0:T(8,128)S(1)}) %tuple.69, (s32[1,512]{1,0:T(1,128)S(1)}, s32[1,1,64]{2,1,0:T(1,128)S(1)}, ...), branch_computations={%region_4.4_spmd, %region_5.7_spmd} | conditional | flops 1146129408 | bytes 17668416 | solution.py:101
  99.0 1.1 constant_dynamic-slice_fusion
  100.1 0.1 broadcast_compare_fusion
  100.2 2.5 %fusion.2 = (f32[64,16]{0,1:T(8,128)S(1)}, f32[512,64,16]{0,1,2:T(8,128)S(1)}) fusion(pred[64,512]{1,0:T(8,128)(4,1)S(1)} %broadcast_compare_fusion, bf16[1,64,16,576]{3,1,2,0:T(8,128)(2,1)} %get-tuple-element.279, bf16[1,1,512,576]{2,3,1,0:T(8,128)(2,1)S(1)} %constant_dynamic-slice_fusion), kind=kOutput, calls=%fused_computation.5 | convolution fusion | flops 605551616 | bytes 3903488 | tf_op jit(solution)/shard_map/while/body/eval_jaxpr/cond/branch_1_fun/pqhe,pke->pqhk/dot_general | solution.py:73
  102.8 0.7 fusion.5
  103.5 0.1 copy.52
  103.6 2.1 copy.53
  105.7 2.2 %bitcast_add_fusion = f32[1,64,16,512]{3,2,1,0:T(8,128)S(1)} fusion(f32[1,64,16,512]{3,2,1,0:T(8,128)S(1)} %get-tuple-element.281, bf16[64,16,512]{2,0,1:T(8,128)(2,1)S(1)} %get-tuple-element.380, f32[64,16]{1,0:T(8,128)S(1)} %copy.52, bf16[1,512,576]{2,1,0:T(8,128)(2,1)} %bitcast.99), kind=kOutput, calls=%fused_computation.2 | convolution fusion | flops 537919488 | bytes 5771264 | tf_op jit(solution)/shard_map/while/body/eval_jaxpr/cond/branch_1_fun/pqhk,pkl->pqhl/dot_general | solution.py:81
  108.0 0.6 fusion.55
  108.6 0.6 iota_add_fusion.2
  109.2 0.5 slice.101
  111.0 0.6 fusion.55
  111.6 0.6 iota_add_fusion.2
  112.2 0.5 slice.101
  114.0 0.6 fusion.55
  114.6 0.6 iota_add_fusion.2
  115.2 0.5 slice.101
  117.1 0.2 fusion.30
  117.3 2.4 %fusion.26 = bf16[1,64,16,128]{3,1,2,0:T(8,128)(2,1)S(1)} fusion(bf16[512,16,256]{0,2,1:T(8,128)(2,1)} %bitcast.103, bf16[64,16,512]{2,1,0:T(8,128)(2,1)S(1)} %fusion.30), kind=kOutput, calls=%fused_computation.34 | convolution fusion | flops 134348800 | bytes 3407872 | tf_op jit(solution)/shard_map/pqhl,lhv->pqhv/dot_general | solution.py:105
  119.7 0.2 copy.74
  119.9 91.0 %all-gather.5.cloned.1.call-done = bf16[2048,2048]{1,0:T(8,128)(2,1)} async-done(((bf16[256,2048]{1,0:T(8,128)(2,1)}), bf16[2048,2048]{1,0:T(8,128)(2,1)}) %all-gather.5.cloned.1.call-update) | async-done | bytes 8388624 | tf_op jit(solution)/shard_map/all_gather | solution.py:109
  210.9 5.7 %fusion.12 = bf16[1,1,64,2048]{3,2,1,0:T(8,128)(2,1)} fusion(bf16[2048,2048]{1,0:T(8,128)(2,1)} %all-gather.5.cloned.1.call-done, bf16[8,8,16,128]{3,2,1,0:T(8,128)(2,1)S(1)} %bitcast.105), kind=kOutput, calls=%fused_computation.24 | convolution fusion | flops 537001984 | bytes 8912896 | tf_op jit(solution)/shard_map/dot_general | solution.py:110
  (41 shorter events, 0.6 us)
Async XLA Ops:
  7.2 6.7 %copy-start.5 = (bf16[1,1,64,576]{3,2,1,0:T(8,128)(2,1)S(1)}, bf16[1,1,64,576]{3,2,1,0:T(8,128)(2,1)}, u32[]{:S(2)}) copy-start(bf16[1,1,64,576]{3,2,1,0:T(8,128)(2,1)} %param.13) | copy-start | bytes 221188
  7.2 6.7 %copy-start.6 = (bf16[512]{0:T(512)(128)(2,1)S(1)}, bf16[512]{0:T(512)(128)(2,1)}, u32[]{:S(2)}) copy-start(bf16[512]{0:T(512)(128)(2,1)} %param.17) | copy-start | bytes 3076
  7.2 78.5 %all-gather.3.cloned.1.call-start = ((), (), s32[]{:S(2)}) async-start(), calls=%async_computation | async-start | bytes 4718592 | tf_op jit(solution)/shard_map/all_gather | solution.py:55
  7.9 27.3 %copy-start.4 = (bf16[1,1,64,3072]{3,2,1,0:T(8,128)(2,1)S(1)}, bf16[1,1,64,3072]{3,2,1,0:T(8,128)(2,1)}, u32[]{:S(2)}) copy-start(bf16[1,1,64,3072]{3,2,1,0:T(8,128)(2,1)} %param.12) | copy-start | bytes 1179652
  7.9 202.9 %all-gather.5.cloned.1.call-start = ((), (), s32[]{:S(2)}) async-start(), calls=%async_computation.1 | async-start | bytes 9437184 | tf_op jit(solution)/shard_map/all_gather | solution.py:109
  15.7 19.6 %copy-start.3 = (bf16[1,1,512,576]{2,3,1,0:T(8,128)(2,1)}, bf16[1,1,512,576]{2,3,1,0:T(8,128)(2,1)S(1)}, u32[]{:S(2)}) copy-start(bf16[1,1,512,576]{2,3,1,0:T(8,128)(2,1)S(1)} %copy.59) | copy-start | bytes 1769476
  15.7 10.0 %collective-permute-start = (bf16[1,1,512,576]{2,3,1,0:T(8,128)(2,1)S(1)}, bf16[1,1,512,576]{2,3,1,0:T(8,128)(2,1)S(1)}, u32[]{:S(2)}, u32[]{:S(2)}) collective-permute-start(bf16[1,1,512,576]{2,3,1,0:T(8,128)(2,1)S(1)} %copy.59), channel_id=1, source_target_pairs={{0,8},{8,16},{16,24},{24,0},{1,9},{9,17},{17,25},{25,1},{2,10},{10... | collective-permute-start | bytes 1769480 | tf_op jit(solution)/shard_map/ppermute | solution.py:19
  25.7 9.3 %collective-permute-start.1 = (bf16[1,1,512,576]{2,3,1,0:T(8,128)(2,1)S(1)}, bf16[1,1,512,576]{2,3,1,0:T(8,128)(2,1)S(1)}, u32[]{:S(2)}, u32[]{:S(2)}) collective-permute-start(bf16[1,1,512,576]{2,3,1,0:T(8,128)(2,1)S(1)} %collective-permute-done), channel_id=1, source_target_pairs={{0,8},{8,16},{16,24},{24,0},{1,9},{9,17},{17,25},{25,1},{2,10},{10... | collective-permute-start | bytes 1769480 | tf_op jit(solution)/shard_map/ppermute | solution.py:19
  35.0 9.4 %collective-permute-start.2 = (bf16[1,1,512,576]{2,3,1,0:T(8,128)(2,1)S(1)}, bf16[1,1,512,576]{2,3,1,0:T(8,128)(2,1)}, u32[]{:S(2)}, u32[]{:S(2)}) collective-permute-start(bf16[1,1,512,576]{2,3,1,0:T(8,128)(2,1)S(1)} %collective-permute-done.1), channel_id=1, source_target_pairs={{0,8},{8,16},{16,24},{24,0},{1,9},{9,17},{17,25},{25,1},{2,10},{10... | collective-permute-start | bytes 1769480 | tf_op jit(solution)/shard_map/ppermute | solution.py:19
  35.9 2.0 copy-start.1
  49.4 42.8 %slice-start = ((bf16[1,1,64,16,192]{4,3,2,1,0:T(8,128)(2,1)}), bf16[1,1,64,16,128]{4,3,2,1,0:T(8,128)(2,1)S(1)}, s32[]{:S(2)}) async-start(bf16[1,1,64,16,192]{4,3,2,1,0:T(8,128)(2,1)} %copy-done.1), calls=%async_computation.2 | async-start | bytes 524288 | tf_op jit(solution)/shard_map/slice | solution.py:58
  92.1 2.3 %copy-start.2 = (bf16[1,1,64,16,32]{4,2,3,1,0:T(8,128)(2,1)S(1)}, bf16[1,1,64,16,32]{4,2,3,1,0:T(8,128)(2,1)}, u32[]{:S(2)}) copy-start(bf16[1,1,64,16,32]{4,2,3,1,0:T(8,128)(2,1)} %get-tuple-element.385) | copy-start | bytes 196612
  94.4 1.6 copy-start.7
  100.1 2.6 %copy-start = (bf16[1,1,512,576]{2,3,1,0:T(8,128)(2,1)}, bf16[1,1,512,576]{2,3,1,0:T(8,128)(2,1)S(1)}, u32[]{:S(2)}) copy-start(bf16[1,1,512,576]{2,3,1,0:T(8,128)(2,1)S(1)} %constant_dynamic-slice_fusion) | copy-start | bytes 1769476 | tf_op jit(solution)/shard_map/while/body/eval_jaxpr/cond
Sparse Core Ops, SparseCore 0:
  10.1 75.5 all-gather.2
  87.8 123.0 all-gather.4
